TPU v7x, 32 devices: a whole 2x2x4 slice. The times are simulated.
32 devices in a mesh: blk: 32 (over z, y, x, core).
Axes of the slice: x: 2, y: 2, z: 4, core: 2. Of those that a mesh axis runs over, the one named last changes fastest.
Arguments:
- tiles: float32 [128, 3, 256, 256], P('blk'), may hold values from -0.109375 to 0.109375
- offsets: int32 [128, 3], P('blk'), may hold values from -2 to 2, as said below
- start: float32 [32768, 128], P('blk'), may hold values from -6 to 6
Outputs:
- grams: float32 [2, 8, 8, 128], replicated
- final: float32 [32768, 128], P('blk')
Inputs may be any that keep to these rules, and one draw needn't show every extreme that they name: The 3 offsets of a block row are all different.
All inputs are finite; a program needn't handle non-finite values.
Results may differ from a plain program's by a relative error of at most 0.00018.
Values sent between devices are 32-bit elements; how exact they have to be, the bound alone decides.
A program may use at most 128 MiB of HBM per device.

v0:
```python
import jax
import jax.numpy as jnp
from jax import lax
from jax.sharding import PartitionSpec as P

TILE = 256
REACH = 2
OUTER = 2
DEPTH = 4


HIGHEST = lax.Precision.HIGHEST


def with_halo(value, sides, width):
    for axis, dim in sides:
        count, length = (lax.axis_size(axis), value.shape[dim])
        up = [(i, (i + 1) % count) for i in range(count)]
        down = [(j, i) for i, j in up]
        last = lax.slice_in_dim(value, length - width, length, axis=dim)
        initial = lax.slice_in_dim(value, 0, width, axis=dim)
        before = lax.ppermute(last, axis, up)
        after = lax.ppermute(initial, axis, down)
        value = jnp.concatenate([before, value, after], axis=dim)
    return value


def pair_products(ext_tiles, ext_offsets, field):
    nblk = ext_tiles.shape[0] - 2 * REACH
    probes = field.shape[1]
    blocks = field.reshape(nblk, TILE, probes)
    padded = with_halo(blocks, (("blk", 0),), 2 * REACH)
    rows_ext = jnp.arange(nblk + 2 * REACH, dtype=jnp.int32)[:, None]
    picked = jnp.take(padded, rows_ext + REACH + ext_offsets, axis=0)
    image_ext = jnp.einsum("rkab,rkbp->rap", ext_tiles, picked, precision=HIGHEST)
    parts = jnp.einsum("rkab,rap->rkbp", ext_tiles, image_ext, precision=HIGHEST)
    spots = jnp.arange(nblk, dtype=jnp.int32) + REACH
    placer = (spots[:, None, None] == (rows_ext + ext_offsets)[None]).astype(jnp.float32)
    total = jnp.einsum("erk,rkbp->ebp", placer, parts, precision=HIGHEST)
    image = image_ext[REACH : REACH + nblk]
    return (image.reshape(field.shape), total.reshape(field.shape))


def gram_total(basis_p, basis_q, total_rows):
    stack = jnp.stack(basis_p + basis_q)
    local = jnp.einsum("arp,brp->abp", stack, stack, precision=HIGHEST)
    return lax.psum(local, "blk") / total_rows


def build_basis(pair, current):
    basis_p = [current]
    basis_q = []
    for depth in range(DEPTH):
        image, after = pair(basis_p[-1])
        basis_q.append(image)
        basis_p.append(after)
    return (basis_p, basis_q)


def on_device(tiles, offsets, start):
    total_rows = start.shape[0] * lax.axis_size("blk")
    ext_tiles = with_halo(tiles, (("blk", 0),), REACH)
    ext_offsets = with_halo(offsets, (("blk", 0),), REACH)

    def pair(field):
        return pair_products(ext_tiles, ext_offsets, field)

    grams = []
    current = start
    for outer in range(OUTER):
        basis_p, basis_q = build_basis(pair, current)
        gram = gram_total(basis_p[:DEPTH], basis_q, total_rows)
        grams.append(gram)
        current = basis_p[DEPTH] / jnp.sqrt(gram[-1, -1] + 0.25)
    return (jnp.stack(grams), current)


def solution(mesh):
    placed = (P("blk", None, None, None), P("blk", None), P("blk", None))
    return jax.shard_map(
        on_device, mesh=mesh, in_specs=placed, out_specs=(P(), P("blk", None)), check_vma=False
    )
```

profile of v0, /device:TPU:0, one launch (start us, length us, event | category | flops | bytes accessed | tf_op | source)
XLA Modules:
  0.0 537.3 jit_solution(11889761041567813648)
XLA Ops:
  11.6 23.3 %collective-permute-done = s32[2,3]{1,0:T(2,128)S(1)} collective-permute-done((s32[2,3]{1,0:T(2,128)S(1)}, s32[2,3]{1,0:T(2,128)S(1)}, u32[]{:S(2)}, u32[]{:S(2)}) %collective-permute-start) | collective-permute-done | bytes 56 | tf_op jit(solution)/shard_map/ppermute | solution.py:22
  34.9 18.9 %collective-permute-done.1 = s32[2,3]{1,0:T(2,128)S(1)} collective-permute-done((s32[2,3]{1,0:T(2,128)S(1)}, s32[2,3]{1,0:T(2,128)S(1)}, u32[]{:S(2)}, u32[]{:S(2)}) %collective-permute-start.1) | collective-permute-done | bytes 56 | tf_op jit(solution)/shard_map/ppermute | solution.py:23
  67.3 10.6 %fusion.121 = f32[8,3,256,128]{3,2,1,0:T(8,128)S(1)} fusion(f32[8,3,256,256]{3,2,1,0:T(8,128)S(1)} %constant_dynamic-update-slice_fusion, f32[8,256,128,1]{2,1,3,0:T(8,128)S(1)} %fusion.30), kind=kOutput, calls=%fused_computation.148 | convolution fusion | flops 2415919104 | bytes 10485760 | tf_op jit(solution)/shard_map/rkab,rap->rkbp/dot_general | solution.py:36
  86.1 6.7 %collective-permute-done.7 = f32[4,256,128]{2,0,1:T(4,128)S(1)} collective-permute-done((f32[4,256,128]{2,0,1:T(4,128)S(1)}, f32[4,256,128]{2,0,1:T(4,128)S(1)}, u32[]{:S(2)}, u32[]{:S(2)}) %collective-permute-start.7) | collective-permute-done | bytes 524320 | tf_op jit(solution)/shard_map/ppermute | solution.py:23
  104.4 10.1 %fusion.28 = f32[8,256,128,1]{2,1,3,0:T(8,128)S(1)} fusion(f32[8,3,256,256]{3,2,1,0:T(8,128)} %copy-done, f32[8,3,256,128]{3,2,1,0:T(8,128)} %bitcast.180, pred[8,3]{1,0:T(8,128)(4,1)S(1)} %get-tuple-element.7), kind=kOutput, calls=%fused_computation.36 | convolution fusion | flops 2416705536 | bytes 10485784 | tf_op jit(solution)/shard_map/rkab,rkbp->rap/dot_general | solution.py:35
  114.6 10.2 %fusion.122 = f32[8,3,256,128]{3,2,1,0:T(8,128)S(1)} fusion(f32[8,3,256,256]{3,2,1,0:T(8,128)S(1)} %bitcast.165, f32[8,256,128,1]{2,1,3,0:T(8,128)S(1)} %fusion.28), kind=kOutput, calls=%fused_computation.149 | convolution fusion | flops 2415919104 | bytes 10485760 | tf_op jit(solution)/shard_map/rkab,rap->rkbp/dot_general | solution.py:36
  147.2 9.9 %fusion.26 = f32[8,256,128,1]{2,1,3,0:T(8,128)S(1)} fusion(f32[8,3,256,256]{3,2,1,0:T(8,128)} %copy-done, f32[8,3,256,128]{3,2,1,0:T(8,128)} %bitcast.181, pred[8,3]{1,0:T(8,128)(4,1)S(1)} %get-tuple-element.7), kind=kOutput, calls=%fused_computation.34 | convolution fusion | flops 2416705536 | bytes 10485784 | tf_op jit(solution)/shard_map/rkab,rkbp->rap/dot_general | solution.py:35
  157.1 10.2 %fusion.123 = f32[8,3,256,128]{3,2,1,0:T(8,128)S(1)} fusion(f32[8,3,256,256]{3,2,1,0:T(8,128)S(1)} %bitcast.167, f32[8,256,128,1]{2,1,3,0:T(8,128)S(1)} %fusion.26), kind=kOutput, calls=%fused_computation.150 | convolution fusion | flops 2415919104 | bytes 10485760 | tf_op jit(solution)/shard_map/rkab,rap->rkbp/dot_general | solution.py:36
  192.3 10.1 %fusion.24 = f32[8,256,128,1]{2,1,3,0:T(8,128)S(1)} fusion(f32[8,3,256,256]{3,2,1,0:T(8,128)} %copy-done, f32[8,3,256,128]{3,2,1,0:T(8,128)} %bitcast.182, pred[8,3]{1,0:T(8,128)(4,1)S(1)} %get-tuple-element.7), kind=kOutput, calls=%fused_computation.32 | convolution fusion | flops 2416705536 | bytes 10485784 | tf_op jit(solution)/shard_map/rkab,rkbp->rap/dot_general | solution.py:35
  202.5 11.7 %fusion.124 = f32[8,3,256,128]{3,2,1,0:T(8,128)} fusion(f32[8,3,256,256]{3,2,1,0:T(8,128)S(1)} %bitcast.169, f32[8,256,128,1]{2,1,3,0:T(8,128)S(1)} %fusion.24), kind=kOutput, calls=%fused_computation.151 | convolution fusion | flops 2415919104 | bytes 10485760 | tf_op jit(solution)/shard_map/rkab,rap->rkbp/dot_general | solution.py:36
  214.7 12.0 %stack.20 = f32[8,1024,128]{1,0,2:T(8,128)} concatenate(f32[1,1024,128]{1,0,2:T(1,128)S(1)} %copy-done.15, f32[1,1024,128]{1,0,2:T(1,128)} %copy.120, f32[1,1024,128]{1,0,2:T(1,128)} %copy.121, f32[1,1024,128]{1,0,2:T(1,128)} %copy.122, f32[1,1024,128]{1,0,2:T(1,128)S(1)} %copy.123, f32[1,1024,128]{1,0,2:T(1,128)} %copy.124, f32[1,1024,128]{1,0,2:T(1,128)} %copy.125, ...), dimensions={0} | concatenate | bytes 8388608 | tf_op jit(solution)/shard_map/stack | solution.py:45
  226.7 12.1 %convolution_bitcast_fusion.1 = f32[8,8,128]{0,1,2:T(8,128)} fusion(f32[8,1024,128]{1,0,2:T(8,128)} %stack.20), kind=kOutput, calls=%fused_computation.73 | convolution fusion | flops 100663296 | bytes 4227072 | tf_op jit(solution)/shard_map/arp,brp->abp/dot_general | solution.py:46
  238.8 47.9 %psum.14 = f32[8,8,128]{0,1,2:T(8,128)} all-reduce(f32[8,8,128]{0,1,2:T(8,128)} %convolution_bitcast_fusion.1), channel_id=1, replica_groups=mesh['blk'=32] {'blk'}, use_global_device_ids=true, to_apply=%region_0.0 | all-reduce | flops 8192 | bytes 65536 | tf_op jit(solution)/shard_map/psum | solution.py:47
  313.2 10.1 %fusion.22 = f32[8,256,128,1]{2,1,3,0:T(8,128)S(1)} fusion(f32[8,3,256,256]{3,2,1,0:T(8,128)} %copy-done, f32[8,3,256,128]{3,2,1,0:T(8,128)} %bitcast.183, pred[8,3]{1,0:T(8,128)(4,1)S(1)} %get-tuple-element.7), kind=kOutput, calls=%fused_computation.30 | convolution fusion | flops 2416705536 | bytes 10485784 | tf_op jit(solution)/shard_map/rkab,rkbp->rap/dot_general | solution.py:35
  323.4 10.2 %fusion.125 = f32[8,3,256,128]{3,2,1,0:T(8,128)S(1)} fusion(f32[8,3,256,256]{3,2,1,0:T(8,128)S(1)} %bitcast.171, f32[8,256,128,1]{2,1,3,0:T(8,128)S(1)} %fusion.22), kind=kOutput, calls=%fused_computation.152 | convolution fusion | flops 2415919104 | bytes 10485760 | tf_op jit(solution)/shard_map/rkab,rap->rkbp/dot_general | solution.py:36
  356.0 9.6 %fusion.20 = f32[8,256,128,1]{2,1,3,0:T(8,128)S(1)} fusion(f32[8,3,256,256]{3,2,1,0:T(8,128)} %copy-done, f32[8,3,256,128]{3,2,1,0:T(8,128)} %bitcast.184, pred[8,3]{1,0:T(8,128)(4,1)S(1)} %get-tuple-element.7), kind=kOutput, calls=%fused_computation.28 | convolution fusion | flops 2416705536 | bytes 10485784 | tf_op jit(solution)/shard_map/rkab,rkbp->rap/dot_general | solution.py:35
  365.7 10.2 %fusion.126 = f32[8,3,256,128]{3,2,1,0:T(8,128)S(1)} fusion(f32[8,3,256,256]{3,2,1,0:T(8,128)S(1)} %bitcast.173, f32[8,256,128,1]{2,1,3,0:T(8,128)S(1)} %fusion.20), kind=kOutput, calls=%fused_computation.153 | convolution fusion | flops 2415919104 | bytes 10485760 | tf_op jit(solution)/shard_map/rkab,rap->rkbp/dot_general | solution.py:36
  399.0 10.3 %fusion.18 = f32[8,256,128,1]{2,1,3,0:T(8,128)S(1)} fusion(f32[8,3,256,256]{3,2,1,0:T(8,128)} %copy-done, f32[8,3,256,128]{3,2,1,0:T(8,128)} %bitcast.185, pred[8,3]{1,0:T(8,128)(4,1)S(1)} %get-tuple-element.7), kind=kOutput, calls=%fused_computation.26 | convolution fusion | flops 2416705536 | bytes 10485784 | tf_op jit(solution)/shard_map/rkab,rkbp->rap/dot_general | solution.py:35
  409.4 10.2 %fusion.127 = f32[8,3,256,128]{3,2,1,0:T(8,128)S(1)} fusion(f32[8,3,256,256]{3,2,1,0:T(8,128)S(1)} %bitcast.175, f32[8,256,128,1]{2,1,3,0:T(8,128)S(1)} %fusion.18), kind=kOutput, calls=%fused_computation.154 | convolution fusion | flops 2415919104 | bytes 10485760 | tf_op jit(solution)/shard_map/rkab,rap->rkbp/dot_general | solution.py:36
  430.2 7.4 %collective-permute-done.18 = f32[4,256,128]{2,0,1:T(4,128)S(1)} collective-permute-done((f32[4,256,128]{2,0,1:T(4,128)S(1)}, f32[4,256,128]{2,0,1:T(4,128)S(1)}, u32[]{:S(2)}, u32[]{:S(2)}) %collective-permute-start.18) | collective-permute-done | bytes 524320 | tf_op jit(solution)/shard_map/ppermute | solution.py:22
  443.8 9.9 %fusion.16 = f32[8,256,128,1]{2,1,3,0:T(8,128)S(1)} fusion(f32[8,3,256,256]{3,2,1,0:T(8,128)} %copy-done, f32[8,3,256,128]{3,2,1,0:T(8,128)} %bitcast.179, pred[8,3]{1,0:T(8,128)(4,1)S(1)} %get-tuple-element.7), kind=kOutput, calls=%fused_computation.24 | convolution fusion | flops 2416705536 | bytes 10485784 | tf_op jit(solution)/shard_map/rkab,rkbp->rap/dot_general | solution.py:35
  453.8 10.2 %fusion.128 = f32[8,3,256,128]{3,2,1,0:T(8,128)S(1)} fusion(f32[8,3,256,256]{3,2,1,0:T(8,128)S(1)} %bitcast.177, f32[8,256,128,1]{2,1,3,0:T(8,128)S(1)} %fusion.16), kind=kOutput, calls=%fused_computation.155 | convolution fusion | flops 2415919104 | bytes 10485760 | tf_op jit(solution)/shard_map/rkab,rap->rkbp/dot_general | solution.py:36
  473.7 11.2 %convolution_bitcast_fusion = f32[8,8,128]{0,1,2:T(8,128)S(1)} fusion(f32[8,1024,128]{1,0,2:T(8,128)} %copy.143), kind=kOutput, calls=%fused_computation.72 | convolution fusion | flops 100663296 | bytes 4227072 | tf_op jit(solution)/shard_map/arp,brp->abp/dot_general | solution.py:46
  484.8 48.4 %psum.15 = f32[8,8,128]{0,1,2:T(8,128)S(1)} all-reduce(f32[8,8,128]{0,1,2:T(8,128)S(1)} %convolution_bitcast_fusion), channel_id=1, replica_groups=mesh['blk'=32] {'blk'}, use_global_device_ids=true, to_apply=%region_1.3 | all-reduce | flops 8192 | bytes 65536 | tf_op jit(solution)/shard_map/psum | solution.py:47
  (198 shorter events, 193.8 us)
Async XLA Ops:
  4.4 52.3 %collective-permute-start.2 = (f32[2,3,256,256]{3,2,1,0:T(8,128)}, f32[2,3,256,256]{3,2,1,0:T(8,128)}, u32[]{:S(2)}, u32[]{:S(2)}) collective-permute-start(f32[2,3,256,256]{3,2,1,0:T(8,128)} %get-tuple-element.10), channel_id=1, source_target_pairs={{0,1},{1,2},{2,3},{3,4},{4,5},{5,6},{6,7},{7,8},{8,9},{9,10},{10,1... | collective-permute-start | bytes 4718600 | tf_op jit(solution)/shard_map/ppermute | solution.py:22
  4.9 54.4 %collective-permute-start.3 = (f32[2,3,256,256]{3,2,1,0:T(8,128)}, f32[2,3,256,256]{3,2,1,0:T(8,128)}, u32[]{:S(2)}, u32[]{:S(2)}) collective-permute-start(f32[2,3,256,256]{3,2,1,0:T(8,128)} %get-tuple-element.9), channel_id=1, source_target_pairs={{1,0},{2,1},{3,2},{4,3},{5,4},{6,5},{7,6},{8,7},{9,8},{10,9},{11,1... | collective-permute-start | bytes 4718600 | tf_op jit(solution)/shard_map/ppermute | solution.py:23
  10.8 43.3 %collective-permute-start.5 = (f32[4,256,128]{2,1,0:T(8,128)S(1)}, f32[4,256,128]{2,1,0:T(8,128)S(1)}, u32[]{:S(2)}, u32[]{:S(2)}) collective-permute-start(f32[4,256,128]{2,1,0:T(8,128)S(1)} %bitcast.209), channel_id=1, source_target_pairs={{1,0},{2,1},{3,2},{4,3},{5,4},{6,5},{7,6},{8,7},{9,8},{10,9},{11,1... | collective-permute-start | bytes 1572872 | tf_op jit(solution)/shard_map/ppermute | solution.py:23
  11.5 42.6 %collective-permute-start.4 = (f32[4,256,128]{2,1,0:T(8,128)S(1)}, f32[4,256,128]{2,1,0:T(8,128)S(1)}, u32[]{:S(2)}, u32[]{:S(2)}) collective-permute-start(f32[4,256,128]{2,1,0:T(8,128)S(1)} %bitcast.210), channel_id=1, source_target_pairs={{0,1},{1,2},{2,3},{3,4},{4,5},{5,6},{6,7},{7,8},{8,9},{9,10},{10,1... | collective-permute-start | bytes 1572872 | tf_op jit(solution)/shard_map/ppermute | solution.py:22
  11.5 23.4 %collective-permute-start = (s32[2,3]{1,0:T(2,128)S(1)}, s32[2,3]{1,0:T(2,128)S(1)}, u32[]{:S(2)}, u32[]{:S(2)}) collective-permute-start(s32[2,3]{1,0:T(2,128)S(1)} %get-tuple-element.15), channel_id=1, source_target_pairs={{0,1},{1,2},{2,3},{3,4},{4,5},{5,6},{6,7},{7,8},{8,9},{9,10},{10,1... | collective-permute-start | bytes 80 | tf_op jit(solution)/shard_map/ppermute | solution.py:22
  34.9 19.0 %collective-permute-start.1 = (s32[2,3]{1,0:T(2,128)S(1)}, s32[2,3]{1,0:T(2,128)S(1)}, u32[]{:S(2)}, u32[]{:S(2)}) collective-permute-start(s32[2,3]{1,0:T(2,128)S(1)} %get-tuple-element.16), channel_id=1, source_target_pairs={{1,0},{2,1},{3,2},{4,3},{5,4},{6,5},{7,6},{8,7},{9,8},{10,9},{11,1... | collective-permute-start | bytes 80 | tf_op jit(solution)/shard_map/ppermute | solution.py:23
  81.1 17.7 %copy-start.9 = (f32[4,256,128]{2,0,1:T(4,128)}, f32[4,256,128]{2,0,1:T(4,128)S(1)}, u32[]{:S(2)}) copy-start(f32[4,256,128]{2,0,1:T(4,128)S(1)} %fusion.48) | copy-start | bytes 1572868
  81.1 11.7 %collective-permute-start.7 = (f32[4,256,128]{2,0,1:T(4,128)S(1)}, f32[4,256,128]{2,0,1:T(4,128)S(1)}, u32[]{:S(2)}, u32[]{:S(2)}) collective-permute-start(f32[4,256,128]{2,0,1:T(4,128)S(1)} %fusion.48), channel_id=1, source_target_pairs={{1,0},{2,1},{3,2},{4,3},{5,4},{6,5},{7,6},{8,7},{9,8},{10,9},{11,1... | collective-permute-start | bytes 1572872 | tf_op jit(solution)/shard_map/ppermute | solution.py:23
  86.1 12.3 %collective-permute-start.6 = (f32[4,256,128]{2,0,1:T(4,128)S(1)}, f32[4,256,128]{2,0,1:T(4,128)S(1)}, u32[]{:S(2)}, u32[]{:S(2)}) collective-permute-start(f32[4,256,128]{2,0,1:T(4,128)S(1)} %fusion.48), channel_id=1, source_target_pairs={{0,1},{1,2},{2,3},{3,4},{4,5},{5,6},{6,7},{7,8},{8,9},{9,10},{10,1... | collective-permute-start | bytes 1572872 | tf_op jit(solution)/shard_map/ppermute | solution.py:22
  128.7 6.8 %collective-permute-start.9 = (f32[4,256,128]{2,0,1:T(4,128)S(1)}, f32[4,256,128]{2,0,1:T(4,128)S(1)}, u32[]{:S(2)}, u32[]{:S(2)}) collective-permute-start(f32[4,256,128]{2,0,1:T(4,128)S(1)} %fusion.51), channel_id=1, source_target_pairs={{1,0},{2,1},{3,2},{4,3},{5,4},{6,5},{7,6},{8,7},{9,8},{10,9},{11,1... | collective-permute-start | bytes 1572872 | tf_op jit(solution)/shard_map/ppermute | solution.py:23
  128.8 12.3 %collective-permute-start.8 = (f32[4,256,128]{2,0,1:T(4,128)S(1)}, f32[4,256,128]{2,0,1:T(4,128)S(1)}, u32[]{:S(2)}, u32[]{:S(2)}) collective-permute-start(f32[4,256,128]{2,0,1:T(4,128)S(1)} %fusion.51), channel_id=1, source_target_pairs={{0,1},{1,2},{2,3},{3,4},{4,5},{5,6},{6,7},{7,8},{8,9},{9,10},{10,1... | collective-permute-start | bytes 1572872 | tf_op jit(solution)/shard_map/ppermute | solution.py:22
  171.5 13.2 %collective-permute-start.11 = (f32[4,256,128]{2,0,1:T(4,128)}, f32[4,256,128]{2,0,1:T(4,128)}, u32[]{:S(2)}, u32[]{:S(2)}) collective-permute-start(f32[4,256,128]{2,0,1:T(4,128)} %fusion.54), channel_id=1, source_target_pairs={{1,0},{2,1},{3,2},{4,3},{5,4},{6,5},{7,6},{8,7},{9,8},{10,9},{11,1... | collective-permute-start | bytes 1572872 | tf_op jit(solution)/shard_map/ppermute | solution.py:23
  171.5 13.3 %collective-permute-start.10 = (f32[4,256,128]{2,0,1:T(4,128)}, f32[4,256,128]{2,0,1:T(4,128)}, u32[]{:S(2)}, u32[]{:S(2)}) collective-permute-start(f32[4,256,128]{2,0,1:T(4,128)} %fusion.54), channel_id=1, source_target_pairs={{0,1},{1,2},{2,3},{3,4},{4,5},{5,6},{6,7},{7,8},{8,9},{9,10},{10,1... | collective-permute-start | bytes 1572872 | tf_op jit(solution)/shard_map/ppermute | solution.py:22
  188.3 14.2 %slice-start.4 = ((s8[6291456]{0:T(1024)(128)(4,1)}), s8[2097152]{0:T(1024)(128)(4,1)S(1)}, s32[]{:S(2)}) async-start(s8[6291456]{0:T(1024)(128)(4,1)} %bitcast.168), calls=%async_computation.4 | async-start | bytes 4194304
  226.7 63.8 %copy-start.14 = (f32[8,3,256,128]{3,2,1,0:T(8,128)S(1)}, f32[8,3,256,128]{3,2,1,0:T(8,128)}, u32[]{:S(2)}) copy-start(f32[8,3,256,128]{3,2,1,0:T(8,128)} %fusion.124) | copy-start | bytes 9437188
  294.5 7.1 %collective-permute-start.13 = (f32[4,256,128]{2,0,1:T(4,128)S(1)}, f32[4,256,128]{2,0,1:T(4,128)S(1)}, u32[]{:S(2)}, u32[]{:S(2)}) collective-permute-start(f32[4,256,128]{2,0,1:T(4,128)S(1)} %get-tuple-element.17), channel_id=1, source_target_pairs={{1,0},{2,1},{3,2},{4,3},{5,4},{6,5},{7,6},{8,7},{9,8},{10,9},{11,1... | collective-permute-start | bytes 1572872 | tf_op jit(solution)/shard_map/ppermute | solution.py:23
  294.9 12.3 %collective-permute-start.12 = (f32[4,256,128]{2,0,1:T(4,128)S(1)}, f32[4,256,128]{2,0,1:T(4,128)S(1)}, u32[]{:S(2)}, u32[]{:S(2)}) collective-permute-start(f32[4,256,128]{2,0,1:T(4,128)S(1)} %get-tuple-element.17), channel_id=1, source_target_pairs={{0,1},{1,2},{2,3},{3,4},{4,5},{5,6},{6,7},{7,8},{8,9},{9,10},{10,1... | collective-permute-start | bytes 1572872 | tf_op jit(solution)/shard_map/ppermute | solution.py:22
  337.5 6.8 %collective-permute-start.15 = (f32[4,256,128]{2,0,1:T(4,128)S(1)}, f32[4,256,128]{2,0,1:T(4,128)S(1)}, u32[]{:S(2)}, u32[]{:S(2)}) collective-permute-start(f32[4,256,128]{2,0,1:T(4,128)S(1)} %fusion.60), channel_id=1, source_target_pairs={{1,0},{2,1},{3,2},{4,3},{5,4},{6,5},{7,6},{8,7},{9,8},{10,9},{11,1... | collective-permute-start | bytes 1572872 | tf_op jit(solution)/shard_map/ppermute | solution.py:23
  337.5 12.4 %collective-permute-start.14 = (f32[4,256,128]{2,0,1:T(4,128)S(1)}, f32[4,256,128]{2,0,1:T(4,128)S(1)}, u32[]{:S(2)}, u32[]{:S(2)}) collective-permute-start(f32[4,256,128]{2,0,1:T(4,128)S(1)} %fusion.60), channel_id=1, source_target_pairs={{0,1},{1,2},{2,3},{3,4},{4,5},{5,6},{6,7},{7,8},{8,9},{9,10},{10,1... | collective-permute-start | bytes 1572872 | tf_op jit(solution)/shard_map/ppermute | solution.py:22
  379.2 7.2 %collective-permute-start.17 = (f32[4,256,128]{2,0,1:T(4,128)S(1)}, f32[4,256,128]{2,0,1:T(4,128)}, u32[]{:S(2)}, u32[]{:S(2)}) collective-permute-start(f32[4,256,128]{2,0,1:T(4,128)S(1)} %fusion.63), channel_id=1, source_target_pairs={{1,0},{2,1},{3,2},{4,3},{5,4},{6,5},{7,6},{8,7},{9,8},{10,9},{11,1... | collective-permute-start | bytes 1572872 | tf_op jit(solution)/shard_map/ppermute | solution.py:23
  379.2 12.5 %collective-permute-start.16 = (f32[4,256,128]{2,0,1:T(4,128)S(1)}, f32[4,256,128]{2,0,1:T(4,128)}, u32[]{:S(2)}, u32[]{:S(2)}) collective-permute-start(f32[4,256,128]{2,0,1:T(4,128)S(1)} %fusion.63), channel_id=1, source_target_pairs={{0,1},{1,2},{2,3},{3,4},{4,5},{5,6},{6,7},{7,8},{8,9},{9,10},{10,1... | collective-permute-start | bytes 1572872 | tf_op jit(solution)/shard_map/ppermute | solution.py:22
  395.0 14.4 %slice-start.10 = ((s8[6291456]{0:T(1024)(128)(4,1)}), s8[2097152]{0:T(1024)(128)(4,1)S(1)}, s32[]{:S(2)}) async-start(s8[6291456]{0:T(1024)(128)(4,1)} %bitcast.174), calls=%async_computation.10 | async-start | bytes 4194304
  423.5 6.8 %collective-permute-start.19 = (f32[4,256,128]{2,0,1:T(4,128)S(1)}, f32[4,256,128]{2,0,1:T(4,128)S(1)}, u32[]{:S(2)}, u32[]{:S(2)}) collective-permute-start(f32[4,256,128]{2,0,1:T(4,128)S(1)} %fusion.66), channel_id=1, source_target_pairs={{1,0},{2,1},{3,2},{4,3},{5,4},{6,5},{7,6},{8,7},{9,8},{10,9},{11,1... | collective-permute-start | bytes 1572872 | tf_op jit(solution)/shard_map/ppermute | solution.py:23
  423.6 14.1 %collective-permute-start.18 = (f32[4,256,128]{2,0,1:T(4,128)S(1)}, f32[4,256,128]{2,0,1:T(4,128)S(1)}, u32[]{:S(2)}, u32[]{:S(2)}) collective-permute-start(f32[4,256,128]{2,0,1:T(4,128)S(1)} %fusion.66), channel_id=1, source_target_pairs={{0,1},{1,2},{2,3},{3,4},{4,5},{5,6},{6,7},{7,8},{8,9},{9,10},{10,1... | collective-permute-start | bytes 1572872 | tf_op jit(solution)/shard_map/ppermute | solution.py:22
  (31 other events, 289.2 us)
where the time goes:
time: 548 us; the launch traced here: 537 us
  matrix products  212 us (39%)
  waiting for transfers between devices  104 us (19%)
  blocking collectives  96.3 us (18%)
  local copies, waits for them, and re-layouts  92 us (17%)
  starting transfers between devices  17 us (3%)
  other arithmetic  13.8 us (3%)
    psum x2, blocking collectives, gram_total(): return lax.psum(local, 'blk') / total_rows  96.3 us
    dot_general x8, matrix products, pair_products(): jnp.einsum('rkab,rap->rkbp', ext_tiles, image_ext, precision=HIGHEST)  83.7 us
    dot_general x8, matrix products, pair_products(): jnp.einsum('rkab,rkbp->rap', ext_tiles, picked, precision=HIGHEST)  75.8 us
    ppermute x10, waiting for transfers between devices, with_halo(): before = lax.ppermute(last, axis, up)  58.6 us
    ppermute x10, waiting for transfers between devices, with_halo(): after = lax.ppermute(initial, axis, down)  45.7 us
    gather x8, local copies, waits for them, and re-layouts, pair_products(): picked = jnp.take(padded, rows_ext + REACH + ext_offsets, axis=0)  30.7 us
    dot_general x8, matrix products, pair_products(): total = jnp.einsum('erk,rkbp->ebp', placer, parts, precision=HIGHEST)  29.3 us
    another operation x11, local copies, waits for them, and re-layouts, gram_total(): stack = jnp.stack(basis_p + basis_q)  27.4 us
  transfers between devices with their start and end apart: 20, of which 14 were waited for; matrix products, arithmetic and copies ran while one was open for 5% of the time, Pallas kernels for 0%

commit v1 on v0

v1 whole, which is shorter than its diff:
```python
import functools

import jax
import jax.numpy as jnp
from jax import lax
from jax.experimental import pallas as pl
from jax.experimental.pallas import tpu as pltpu
from jax.sharding import PartitionSpec as P

REACH = 2
OUTER = 2
DEPTH = 4
MESH = pl.DeviceIdType.MESH
F32 = jnp.float32
BF16 = jnp.bfloat16


def halves(x):
    high = x.astype(BF16)
    return high, (x - high.astype(F32)).astype(BF16)


def kernel(
    n,
    levels,
    total_rows,
    off_ref,
    tiles_hbm,
    start_hbm,
    gram_ref,
    final_ref,
    raw,
    fwd,
    adj,
    basis,
    field,
    image,
    parts,
    halo_l,
    halo_r,
    give_l,
    give_r,
    part_l,
    part_r,
    gram,
    sums,
    heard,
    load_sem,
    send_sem,
    recv_sem,
    sum_send,
    sum_recv,
):
    nblk, slots, tile, _ = raw.shape
    probes = basis.shape[2]
    edge = REACH * tile
    me = lax.axis_index("blk")
    left, right = lax.rem(me + n - 1, n), lax.rem(me + 1, n)
    partners = []
    for b in range(levels):
        s = 1 << b
        partners.append(me + s * (1 - 2 * lax.rem(me // s, 2)))

    load_start = pltpu.make_async_copy(start_hbm, basis.at[0], load_sem.at[0])
    load_start.start()
    load_tiles = pltpu.make_async_copy(tiles_hbm, raw, load_sem.at[1])
    load_tiles.start()

    barrier = pltpu.get_barrier_semaphore()
    for other in [left, right] + partners:
        pl.semaphore_signal(barrier, inc=1, device_id=(other,), device_id_type=MESH)

    def remote(src, dst, k, device):
        return pltpu.make_async_remote_copy(
            src_ref=src,
            dst_ref=dst,
            send_sem=send_sem.at[k],
            recv_sem=recv_sem.at[k],
            device_id=(device,),
            device_id_type=MESH,
        )

    def edges(t):
        return (
            remote(basis.at[t, pl.ds(0, edge)], halo_r, 0, left),
            remote(basis.at[t, pl.ds(nblk * tile - edge, edge)], halo_l, 1, right),
        )

    def give():
        return remote(give_l, part_r, 2, left), remote(give_r, part_l, 3, right)

    def sum_step(outer, b):
        k = outer * levels + b
        return pltpu.make_async_remote_copy(
            src_ref=sums.at[outer * (levels + 1) + b],
            dst_ref=heard.at[k],
            send_sem=sum_send.at[k],
            recv_sem=sum_recv.at[k],
            device_id=(partners[b],),
            device_id_type=MESH,
        )

    where = [[i + REACH + off_ref[i, k] for k in range(slots)] for i in range(nblk)]
    source = {}
    for i in range(nblk):
        for d in range(-REACH, REACH + 1):
            index = nblk * slots
            for k in range(slots):
                index = jnp.where(off_ref[i, k] == d, i * slots + k, index)
            source[i, d] = index

    gram[...] = jnp.zeros_like(gram)
    parts[nblk * slots] = jnp.zeros((tile, probes), F32)

    load_start.wait()
    pl.semaphore_wait(barrier, 2 + levels)
    for copy in edges(0):
        copy.start()
    load_tiles.wait()

    def prepare(i, carry):
        for k in range(slots):
            value = raw[i, k]
            high, low = halves(value)
            fwd[i, pl.ds(0, tile), pl.ds(k * tile, tile)] = high
            fwd[i, pl.ds(tile, tile), pl.ds(k * tile, tile)] = low
            high, low = halves(value.T)
            adj[i, pl.ds(2 * k * tile, tile), :] = high
            adj[i, pl.ds((2 * k + 1) * tile, tile), :] = low
        return carry

    lax.fori_loop(0, nblk, prepare, 0)

    def keep(ref, i, value):
        high, low = halves(value)
        ref[i, :, pl.ds(0, probes)] = high
        ref[i, :, pl.ds(probes, probes)] = low

    def joined(r, base):
        top = r[base : base + tile]
        low = r[base + tile : base + 2 * tile]
        return (top[:, :probes] + top[:, probes:]) + (low[:, :probes] + low[:, probes:])

    def gram_rows(t):
        def one(u, carry):
            prod = basis[t] * basis[u]
            s = jnp.sum(prod.reshape(-1, 8, probes), axis=0)
            gram[pl.ds(t * 2 * DEPTH + u, 1), :] = jnp.sum(s, axis=0, keepdims=True)
            return carry

        lax.fori_loop(0, t + 1, one, 0)

    def pair(outer, j, last):
        t = 2 * j
        for i in range(nblk):
            keep(field, i + REACH, basis[t, pl.ds(i * tile, tile), :])
        gram_rows(t)
        for copy in edges(t):
            copy.wait()
        for h in range(REACH):
            keep(field, h, halo_l[pl.ds(h * tile, tile), :])
            keep(field, nblk + REACH + h, halo_r[pl.ds(h * tile, tile), :])
        for i in range(nblk):
            rhs = jnp.concatenate([field[where[i][k]] for k in range(slots)], axis=0)
            q = joined(jnp.dot(fwd[i], rhs, preferred_element_type=F32), 0)
            basis[t + 1, pl.ds(i * tile, tile), :] = q
            keep(image, i, q)
        if last:
            gram_rows(t + 1)
            sums[outer * (levels + 1)] = gram[...]
            sum_step(outer, 0).start()

        def spread(i):
            r = jnp.dot(adj[i], image[i], preferred_element_type=F32)
            for k in range(slots):
                parts[i * slots + k] = joined(r, 2 * k * tile)

        def gathered(target):
            total = None
            for i in range(nblk):
                if abs(target - i) <= REACH:
                    term = parts[source[i, target - i]]
                    total = term if total is None else total + term
            return total

        done = []
        for i in range(min(REACH, nblk)):
            spread(i)
            done.append(i)
        for h in range(REACH):
            give_l[pl.ds(h * tile, tile), :] = gathered(h - REACH)
        to_left, to_right = give()
        to_left.start()
        for i in range(nblk):
            if i not in done:
                spread(i)
        for h in range(REACH):
            give_r[pl.ds(h * tile, tile), :] = gathered(nblk + h)
        to_right.start()
        for i in range(nblk):
            basis[t + 2, pl.ds(i * tile, tile), :] = gathered(i)
        if last:
            for b in range(levels):
                sum_step(outer, b).wait()
                k = outer * (levels + 1) + b
                sums[k + 1] = sums[k] + heard[outer * levels + b]
                if b + 1 < levels:
                    sum_step(outer, b + 1).start()
        else:
            gram_rows(t + 1)
        to_left.wait()
        to_right.wait()
        basis[t + 2, pl.ds(0, edge), :] += part_l[...]
        basis[t + 2, pl.ds(nblk * tile - edge, edge), :] += part_r[...]

    def outer_step(outer, carry):
        def inner(j, c):
            pair(outer, j, False)
            for copy in edges(2 * j + 2):
                copy.start()
            return c

        lax.fori_loop(0, DEPTH - 1, inner, 0)
        pair(outer, DEPTH - 1, True)
        total = outer * (levels + 1) + levels
        size = 2 * DEPTH
        corner = sums[total, pl.ds(size * size - 1, 1), :] / total_rows
        scale = 1.0 / jnp.sqrt(corner + 0.25)
        basis[0] = basis[size] * scale

        @pl.when(outer < OUTER - 1)
        def _():
            for copy in edges(0):
                copy.start()

        when = [2 * a for a in range(DEPTH)] + [2 * a + 1 for a in range(DEPTH)]
        for a in range(size):
            for b in range(size):
                row = max(when[a], when[b]) * size + min(when[a], when[b])
                gram_ref[outer, pl.ds(a * size + b, 1), :] = (
                    sums[total, pl.ds(row, 1), :] / total_rows
                )
        return carry

    lax.fori_loop(0, OUTER, outer_step, 0)
    final_ref[...] = basis[0]


def on_device(tiles, offsets, start):
    n = lax.axis_size("blk")
    levels = n.bit_length() - 1
    assert n == 1 << levels
    nblk, slots, tile, _ = tiles.shape
    rows, probes = start.shape
    edge = REACH * tile
    size = 2 * DEPTH
    dma = pltpu.SemaphoreType.DMA
    grams, final = pl.pallas_call(
        functools.partial(kernel, n, levels, float(rows * n)),
        out_shape=(
            jax.ShapeDtypeStruct((OUTER, size * size, probes), F32),
            jax.ShapeDtypeStruct((rows, probes), F32),
        ),
        in_specs=[
            pl.BlockSpec(memory_space=pltpu.SMEM),
            pl.BlockSpec(memory_space=pl.ANY),
            pl.BlockSpec(memory_space=pl.ANY),
        ],
        out_specs=(pl.BlockSpec(memory_space=pltpu.VMEM), pl.BlockSpec(memory_space=pltpu.VMEM)),
        scratch_shapes=[
            pltpu.VMEM(tiles.shape, F32),
            pltpu.VMEM((nblk, 2 * tile, slots * tile), BF16),
            pltpu.VMEM((nblk, 2 * slots * tile, tile), BF16),
            pltpu.VMEM((size + 1, rows, probes), F32),
            pltpu.VMEM((nblk + 2 * REACH, tile, 2 * probes), BF16),
            pltpu.VMEM((nblk, tile, 2 * probes), BF16),
            pltpu.VMEM((nblk * slots + 1, tile, probes), F32),
        ]
        + [pltpu.VMEM((edge, probes), F32)] * 6
        + [
            pltpu.VMEM((size * size, probes), F32),
            pltpu.VMEM((OUTER * (levels + 1), size * size, probes), F32),
            pltpu.VMEM((OUTER * levels, size * size, probes), F32),
            dma((2,)),
            dma((4,)),
            dma((4,)),
            dma((OUTER * levels,)),
            dma((OUTER * levels,)),
        ],
        compiler_params=pltpu.CompilerParams(collective_id=0, has_side_effects=True),
    )(offsets, tiles, start)
    return grams.reshape(OUTER, size, size, probes), final


def solution(mesh):
    placed = (P("blk", None, None, None), P("blk", None), P("blk", None))
    return jax.shard_map(
        on_device, mesh=mesh, in_specs=placed, out_specs=(P(), P("blk", None)), check_vma=False
    )
```

time: 548 us -> 160 us (0.29); the launches traced: 537 us -> 160 us
  matrix products: 212 us -> 0 us
  Pallas kernels: 0 us -> 156 us
  waiting for transfers between devices: 104 us -> 0 us
  blocking collectives: 96.3 us -> 0 us
  local copies, waits for them, and re-layouts: 92 us -> 3.34 us
  starting transfers between devices: 17 us -> 0 us
  other arithmetic: 13.8 us -> 0 us
    dot_general x26 -> x0, matrix products: 212 us -> none  [the longest x8 83.7 us: pair_products(): jnp.einsum('rkab,rap->rkbp', ext_tiles, image_ext, precision=HIGHEST)]
    pallas_call x0 -> x1, Pallas kernels: none -> 156 us  [on_device(): pl.pallas_call(functools.partial(kernel, n, levels, float(rows * n)), out...]
    ppermute x20 -> x0, waiting for transfers between devices: 104 us -> none  [the longest x10 58.6 us: with_halo(): before = lax.ppermute(last, axis, up)]
    psum x2 -> x0, blocking collectives: 96.3 us -> none  [gram_total(): return lax.psum(local, 'blk') / total_rows]
    gather x8 -> x0, local copies, waits for them, and re-layouts: 30.7 us -> none  [pair_products(): picked = jnp.take(padded, rows_ext + REACH + ext_offsets, axis=0)]
    another operation x13 -> x0, local copies, waits for them, and re-layouts: 28.8 us -> none  [the longest x11 27.4 us: gram_total(): stack = jnp.stack(basis_p + basis_q)]
    ppermute x20 -> x0, starting transfers between devices: 17 us -> none  [the longest x10 12.2 us: with_halo(): after = lax.ppermute(initial, axis, down)]
    concatenate x8 -> x0, local copies, waits for them, and re-layouts: 13.1 us -> none  [with_halo(): value = jnp.concatenate([before, value, after], axis=dim)]
  transfers between devices with their start and end apart: 20 -> 0, of which waited for: 14 -> 0; matrix products, arithmetic and copies ran while one was open for 5% -> 0% of each run, Pallas kernels for 0% -> 0%
where the time goes in v1:
time: 160 us
  Pallas kernels  156 us (98%)
  local copies, waits for them, and re-layouts  3.34 us (2%)
    pallas_call x1, Pallas kernels, on_device(): pl.pallas_call(functools.partial(kernel, n, levels, float(rows * n)), out...  156 us
    unnamed x2, local copies, waits for them, and re-layouts  3.34 us

profile of v1, /device:TPU:0, one launch (start us, length us, event | category | flops | bytes accessed | tf_op | source)
XLA Modules:
  0.0 159.8 jit_solution(8107711237063498827)
XLA Ops:
  0.6 155.8 %shard_map.50 = (f32[2,64,128]{2,1,0:T(8,128)}, f32[1024,128]{1,0:T(8,128)}) custom-call(s32[4,3]{1,0:T(4,128)} %off_ref.1, f32[4,3,256,256]{3,2,1,0:T(8,128)} %tiles_hbm.1, f32[1024,128]{1,0:T(8,128)} %start_hbm.1), custom_call_target="tpu_custom_call" | custom-call | tf_op jit(solution)/shard_map/pallas_call | solution.py:258
  156.5 1.5 copy.7
  158.0 1.9 %copy.8 = f32[1024,128]{1,0:T(8,128)} copy(f32[1024,128]{1,0:T(8,128)} %get-tuple-element.9) | data formatting | bytes 1048576

commit v2 on v1

v2 whole, which is shorter than its diff:
```python
import functools

import jax
import jax.numpy as jnp
from jax import lax
from jax.experimental import pallas as pl
from jax.experimental.pallas import tpu as pltpu
from jax.sharding import PartitionSpec as P

REACH = 2
OUTER = 2
DEPTH = 4
MESH = pl.DeviceIdType.MESH
F32 = jnp.float32
BF16 = jnp.bfloat16


def halves(x):
    high = x.astype(BF16)
    return high, (x - high.astype(F32)).astype(BF16)


def kernel(
    n,
    levels,
    total_rows,
    off_ref,
    tiles_hbm,
    start_hbm,
    gram_ref,
    final_ref,
    raw,
    fwd,
    adj,
    basis,
    field,
    image,
    parts,
    halo,
    give,
    got,
    gram,
    sums,
    heard,
    load_sem,
    send_sem,
    recv_sem,
    sum_send,
    sum_recv,
):
    nblk, slots, tile, _ = raw.shape
    probes = basis.shape[3]
    me = lax.axis_index("blk")
    slow = lax.rem(me, 2)
    fast = 1 - slow
    left, right = lax.rem(me + n - 1, n), lax.rem(me + 1, n)
    partners = []
    for b in range(levels):
        s = 1 << b
        partners.append(me + s * (1 - 2 * lax.rem(me // s, 2)))

    load_start = pltpu.make_async_copy(start_hbm, basis.at[0], load_sem.at[0])
    load_start.start()
    load_tiles = pltpu.make_async_copy(tiles_hbm, raw, load_sem.at[1])
    load_tiles.start()

    barrier = pltpu.get_barrier_semaphore()
    for other in [left, right] + partners:
        pl.semaphore_signal(barrier, inc=1, device_id=(other,), device_id_type=MESH)

    def block(side, k):
        return side * (nblk - 1) + k * (1 - 2 * side)

    def beyond(side, k):
        return side * (nblk + 1 + 2 * k) - 1 - k

    def remote(src, dst, here, there, side):
        return pltpu.make_async_remote_copy(
            src_ref=src,
            dst_ref=dst,
            send_sem=send_sem.at[here],
            recv_sem=recv_sem.at[there],
            device_id=(lax.rem(me + n - 1 + 2 * side, n),),
            device_id_type=MESH,
        )

    def send_p(t, side, k):
        there = (1 - side) * REACH + k
        remote(basis.at[t, block(side, k)], halo.at[there], side * REACH + k, there, side).start()

    def wait_p(t, side, k):
        here = side * REACH + k
        remote(basis.at[t, block(side, k)], halo.at[here], here, here, side).wait()

    def send_part(side, k):
        here, there = side * REACH + k, (1 - side) * REACH + k
        more = 2 * REACH
        remote(give.at[here], got.at[there], more + here, more + there, side).start()

    def wait_part(side, k):
        here = side * REACH + k
        sem = 2 * REACH + here
        remote(give.at[here], got.at[here], sem, sem, side).wait()

    def sum_step(outer, b):
        k = outer * levels + b
        return pltpu.make_async_remote_copy(
            src_ref=sums.at[outer * (levels + 1) + b],
            dst_ref=heard.at[k],
            send_sem=sum_send.at[k],
            recv_sem=sum_recv.at[k],
            device_id=(partners[b],),
            device_id_type=MESH,
        )

    def source(i, d):
        index = nblk * slots
        for k in range(slots):
            index = jnp.where(off_ref[i, k] == d, i * slots + k, index)
        return index

    gram[...] = jnp.zeros_like(gram)
    parts[nblk * slots] = jnp.zeros((tile, probes), F32)

    load_start.wait()
    pl.semaphore_wait(barrier, 2 + levels)
    for k in range(REACH):
        send_p(0, slow, k)
        send_p(0, fast, k)
    load_tiles.wait()

    def prepare(i, carry):
        for k in range(slots):
            value = raw[i, k]
            high, low = halves(value)
            fwd[i, pl.ds(0, tile), pl.ds(k * tile, tile)] = high
            fwd[i, pl.ds(tile, tile), pl.ds(k * tile, tile)] = low
            high, low = halves(value.T)
            adj[i, pl.ds(2 * k * tile, tile), :] = high
            adj[i, pl.ds((2 * k + 1) * tile, tile), :] = low
        return carry

    lax.fori_loop(0, nblk, prepare, 0)

    def keep(ref, i, value):
        high, low = halves(value)
        ref[i, :, pl.ds(0, probes)] = high
        ref[i, :, pl.ds(probes, probes)] = low

    def joined(r, base):
        top = r[base : base + tile]
        low = r[base + tile : base + 2 * tile]
        return (top[:, :probes] + top[:, probes:]) + (low[:, :probes] + low[:, probes:])

    def gram_rows(t):
        def one(u, carry):
            prod = (basis[t] * basis[u]).reshape(-1, probes)
            s = jnp.sum(prod.reshape(-1, 8, probes), axis=0)
            gram[pl.ds(t * 2 * DEPTH + u, 1), :] = jnp.sum(s, axis=0, keepdims=True)
            return carry

        lax.fori_loop(0, t + 1, one, 0)

    def forward(t, i):
        rhs = jnp.concatenate([field[i + REACH + off_ref[i, k]] for k in range(slots)], axis=0)
        q = joined(jnp.dot(fwd[i], rhs, preferred_element_type=F32), 0)
        basis[t + 1, i] = q
        keep(image, i, q)
        r = jnp.dot(adj[i], image[i], preferred_element_type=F32)
        for k in range(slots):
            parts[i * slots + k] = joined(r, 2 * k * tile)

    def arrive(t, side, k):
        wait_p(t, side, k)
        keep(field, beyond(side, k) + REACH, halo[side * REACH + k])

    def hand_over(side):
        for k in range(REACH):
            total = None
            for r in range(REACH - k):
                term = parts[source(block(side, r), (2 * side - 1) * (r + 1 + k))]
                total = term if total is None else total + term
            give[side * REACH + k] = total
            send_part(side, k)

    def gathered(target):
        total = None
        for i in range(nblk):
            if abs(target - i) <= REACH:
                term = parts[source(i, target - i)]
                total = term if total is None else total + term
        return total

    def take(t, side, k, last):
        wait_part(side, k)
        basis[t, block(side, k)] += got[side * REACH + k]
        if not last:
            send_p(t, side, k)

    def pair(outer, j, last):
        t = 2 * j
        for i in range(nblk):
            keep(field, i + REACH, basis[t, i])
        gram_rows(t)
        for k in range(REACH):
            arrive(t, fast, k)
        for i in range(REACH, nblk - REACH):
            forward(t, i)
        for k in reversed(range(REACH)):
            forward(t, block(fast, k))
        hand_over(fast)
        for k in range(REACH):
            arrive(t, slow, k)
            forward(t, block(slow, REACH - 1 - k))
        hand_over(slow)
        if last:
            gram_rows(t + 1)
            sums[outer * (levels + 1)] = gram[...]
            sum_step(outer, 0).start()
        for i in range(nblk):
            basis[t + 2, i] = gathered(i)
        for k in range(REACH):
            take(t + 2, fast, k, last)
        if last:
            for b in range(levels):
                sum_step(outer, b).wait()
                k = outer * (levels + 1) + b
                sums[k + 1] = sums[k] + heard[outer * levels + b]
                if b + 1 < levels:
                    sum_step(outer, b + 1).start()
        else:
            gram_rows(t + 1)
        for k in range(REACH):
            take(t + 2, slow, k, last)

    def outer_step(outer, carry):
        def inner(j, c):
            pair(outer, j, False)
            return c

        lax.fori_loop(0, DEPTH - 1, inner, 0)
        pair(outer, DEPTH - 1, True)
        total = outer * (levels + 1) + levels
        size = 2 * DEPTH
        corner = sums[total, pl.ds(size * size - 1, 1), :] / total_rows
        scale = 1.0 / jnp.sqrt(corner + 0.25)
        basis[0] = basis[size] * scale[None]

        @pl.when(outer < OUTER - 1)
        def _():
            for k in range(REACH):
                send_p(0, slow, k)
                send_p(0, fast, k)

        when = [2 * a for a in range(DEPTH)] + [2 * a + 1 for a in range(DEPTH)]
        for a in range(size):
            for b in range(size):
                row = max(when[a], when[b]) * size + min(when[a], when[b])
                gram_ref[outer, pl.ds(a * size + b, 1), :] = (
                    sums[total, pl.ds(row, 1), :] / total_rows
                )
        return carry

    lax.fori_loop(0, OUTER, outer_step, 0)
    final_ref[...] = basis[0]


def on_device(tiles, offsets, start):
    n = lax.axis_size("blk")
    levels = n.bit_length() - 1
    assert n == 1 << levels
    nblk, slots, tile, _ = tiles.shape
    rows, probes = start.shape
    assert nblk >= 2 * REACH
    size = 2 * DEPTH
    dma = pltpu.SemaphoreType.DMA
    grams, final = pl.pallas_call(
        functools.partial(kernel, n, levels, float(rows * n)),
        out_shape=(
            jax.ShapeDtypeStruct((OUTER, size * size, probes), F32),
            jax.ShapeDtypeStruct((nblk, tile, probes), F32),
        ),
        in_specs=[
            pl.BlockSpec(memory_space=pltpu.SMEM),
            pl.BlockSpec(memory_space=pl.ANY),
            pl.BlockSpec(memory_space=pl.ANY),
        ],
        out_specs=(pl.BlockSpec(memory_space=pltpu.VMEM), pl.BlockSpec(memory_space=pltpu.VMEM)),
        scratch_shapes=[
            pltpu.VMEM(tiles.shape, F32),
            pltpu.VMEM((nblk, 2 * tile, slots * tile), BF16),
            pltpu.VMEM((nblk, 2 * slots * tile, tile), BF16),
            pltpu.VMEM((size + 1, nblk, tile, probes), F32),
            pltpu.VMEM((nblk + 2 * REACH, tile, 2 * probes), BF16),
            pltpu.VMEM((nblk, tile, 2 * probes), BF16),
            pltpu.VMEM((nblk * slots + 1, tile, probes), F32),
        ]
        + [pltpu.VMEM((2 * REACH, tile, probes), F32)] * 3
        + [
            pltpu.VMEM((size * size, probes), F32),
            pltpu.VMEM((OUTER * (levels + 1), size * size, probes), F32),
            pltpu.VMEM((OUTER * levels, size * size, probes), F32),
            dma((2,)),
            dma((4 * REACH,)),
            dma((4 * REACH,)),
            dma((OUTER * levels,)),
            dma((OUTER * levels,)),
        ],
        compiler_params=pltpu.CompilerParams(collective_id=0, has_side_effects=True),
    )(offsets, tiles, start.reshape(nblk, tile, probes))
    return grams.reshape(OUTER, size, size, probes), final.reshape(rows, probes)


def solution(mesh):
    placed = (P("blk", None, None, None), P("blk", None), P("blk", None))
    return jax.shard_map(
        on_device, mesh=mesh, in_specs=placed, out_specs=(P(), P("blk", None)), check_vma=False
    )
```

time: 160 us -> 143 us (0.89)
  Pallas kernels: 156 us -> 139 us
    pallas_call x1, Pallas kernels: 156 us -> 139 us  [on_device(): pl.pallas_call(functools.partial(kernel, n, levels, float(rows * n)), out...]
where the time goes in v2:
time: 143 us
  Pallas kernels  139 us (97%)
  local copies, waits for them, and re-layouts  3.34 us (2%)
    pallas_call x1, Pallas kernels, on_device(): pl.pallas_call(functools.partial(kernel, n, levels, float(rows * n)), out...  139 us
    unnamed x2, local copies, waits for them, and re-layouts  3.34 us

profile of v2, /device:TPU:0, one launch (start us, length us, event | category | flops | bytes accessed | tf_op | source)
XLA Modules:
  0.0 142.8 jit_solution(7383369477594381824)
XLA Ops:
  0.6 138.8 %shard_map.50 = (f32[2,64,128]{2,1,0:T(8,128)}, f32[4,256,128]{2,1,0:T(8,128)}) custom-call(s32[4,3]{1,0:T(4,128)} %off_ref.1, f32[4,3,256,256]{3,2,1,0:T(8,128)} %tiles_hbm.1, f32[4,256,128]{2,1,0:T(8,128)} %bitcast.3), custom_call_target="tpu_custom_call" | custom-call | tf_op jit(solution)/shard_map/pallas_call | solution.py:277
  139.5 1.5 %copy.7 = f32[2,8,8,128]{3,2,1,0:T(8,128)} copy(f32[2,8,8,128]{3,2,1,0:T(8,128)} %bitcast.5) | data formatting | bytes 131072
  140.9 1.9 %copy.8 = f32[1024,128]{1,0:T(8,128)} copy(f32[1024,128]{1,0:T(8,128)} %bitcast.4) | data formatting | bytes 1048576

commit v3 on v2

--- a/solution.py
+++ b/solution.py
@@ -10,6 +10,7 @@
 REACH = 2
 OUTER = 2
 DEPTH = 4
+SPLIT = 2
 MESH = pl.DeviceIdType.MESH
 F32 = jnp.float32
 BF16 = jnp.bfloat16
@@ -84,23 +85,33 @@
             device_id_type=MESH,
         )
 
-    def send_p(t, side, k):
-        there = (1 - side) * REACH + k
-        remote(basis.at[t, block(side, k)], halo.at[there], side * REACH + k, there, side).start()
+    piece = tile // SPLIT
+
+    def span(h):
+        return pl.ds(h * piece, piece)
+
+    def send_p(t, side, k, h):
+        here, there = side * REACH + k, (1 - side) * REACH + k
+        src, dst = basis.at[t, block(side, k), span(h)], halo.at[there, span(h)]
+        remote(src, dst, here * SPLIT + h, there * SPLIT + h, side).start()
 
     def wait_p(t, side, k):
         here = side * REACH + k
-        remote(basis.at[t, block(side, k)], halo.at[here], here, here, side).wait()
-
-    def send_part(side, k):
+        for h in range(SPLIT):
+            src, dst = basis.at[t, block(side, k), span(h)], halo.at[here, span(h)]
+            remote(src, dst, here * SPLIT + h, here * SPLIT + h, side).wait()
+
+    more = 2 * REACH * SPLIT
+
+    def send_part(side, k, h):
         here, there = side * REACH + k, (1 - side) * REACH + k
-        more = 2 * REACH
-        remote(give.at[here], got.at[there], more + here, more + there, side).start()
-
-    def wait_part(side, k):
+        src, dst = give.at[here, span(h)], got.at[there, span(h)]
+        remote(src, dst, more + here * SPLIT + h, more + there * SPLIT + h, side).start()
+
+    def wait_part(side, k, h):
         here = side * REACH + k
-        sem = 2 * REACH + here
-        remote(give.at[here], got.at[here], sem, sem, side).wait()
+        sem = more + here * SPLIT + h
+        remote(give.at[here, span(h)], got.at[here, span(h)], sem, sem, side).wait()
 
     def sum_step(outer, b):
         k = outer * levels + b
@@ -125,8 +136,9 @@
     load_start.wait()
     pl.semaphore_wait(barrier, 2 + levels)
     for k in range(REACH):
-        send_p(0, slow, k)
-        send_p(0, fast, k)
+        for h in range(SPLIT):
+            send_p(0, slow, k, h)
+            send_p(0, fast, k, h)
     load_tiles.wait()
 
     def prepare(i, carry):
@@ -176,12 +188,14 @@
 
     def hand_over(side):
         for k in range(REACH):
-            total = None
-            for r in range(REACH - k):
-                term = parts[source(block(side, r), (2 * side - 1) * (r + 1 + k))]
-                total = term if total is None else total + term
-            give[side * REACH + k] = total
-            send_part(side, k)
+            for h in range(SPLIT):
+                total = None
+                for r in range(REACH - k):
+                    index = source(block(side, r), (2 * side - 1) * (r + 1 + k))
+                    term = parts[index, span(h)]
+                    total = term if total is None else total + term
+                give[side * REACH + k, span(h)] = total
+                send_part(side, k, h)
 
     def gathered(target):
         total = None
@@ -192,10 +206,11 @@
         return total
 
     def take(t, side, k, last):
-        wait_part(side, k)
-        basis[t, block(side, k)] += got[side * REACH + k]
-        if not last:
-            send_p(t, side, k)
+        for h in range(SPLIT):
+            wait_part(side, k, h)
+            basis[t, block(side, k), span(h)] += got[side * REACH + k, span(h)]
+            if not last:
+                send_p(t, side, k, h)
 
     def pair(outer, j, last):
         t = 2 * j
@@ -249,8 +264,9 @@
         @pl.when(outer < OUTER - 1)
         def _():
             for k in range(REACH):
-                send_p(0, slow, k)
-                send_p(0, fast, k)
+                for h in range(SPLIT):
+                    send_p(0, slow, k, h)
+                    send_p(0, fast, k, h)
 
         when = [2 * a for a in range(DEPTH)] + [2 * a + 1 for a in range(DEPTH)]
         for a in range(size):
@@ -301,8 +317,8 @@
             pltpu.VMEM((OUTER * (levels + 1), size * size, probes), F32),
             pltpu.VMEM((OUTER * levels, size * size, probes), F32),
             dma((2,)),
-            dma((4 * REACH,)),
-            dma((4 * REACH,)),
+            dma((4 * REACH * SPLIT,)),
+            dma((4 * REACH * SPLIT,)),
             dma((OUTER * levels,)),
             dma((OUTER * levels,)),
         ],

time: 143 us -> 142 us (level)
  no operation moved by 1% of the time
where the time goes in v3:
time: 142 us
  Pallas kernels  138 us (97%)
  local copies, waits for them, and re-layouts  3.34 us (2%)
    pallas_call x1, Pallas kernels, on_device(): pl.pallas_call(functools.partial(kernel, n, levels, float(rows * n)), out...  138 us
    unnamed x2, local copies, waits for them, and re-layouts  3.34 us

profile of v3, /device:TPU:0, one launch (start us, length us, event | category | flops | bytes accessed | tf_op | source)
XLA Modules:
  0.0 141.7 jit_solution(6489958903953648261)
XLA Ops:
  0.6 137.7 %shard_map.50 = (f32[2,64,128]{2,1,0:T(8,128)}, f32[4,256,128]{2,1,0:T(8,128)}) custom-call(s32[4,3]{1,0:T(4,128)} %off_ref.1, f32[4,3,256,256]{3,2,1,0:T(8,128)} %tiles_hbm.1, f32[4,256,128]{2,1,0:T(8,128)} %bitcast.3), custom_call_target="tpu_custom_call" | custom-call | tf_op jit(solution)/shard_map/pallas_call | solution.py:293
  138.4 1.5 %copy.7 = f32[2,8,8,128]{3,2,1,0:T(8,128)} copy(f32[2,8,8,128]{3,2,1,0:T(8,128)} %bitcast.5) | data formatting | bytes 131072
  139.8 1.9 %copy.8 = f32[1024,128]{1,0:T(8,128)} copy(f32[1024,128]{1,0:T(8,128)} %bitcast.4) | data formatting | bytes 1048576
